TPU v7x, 512 devices: a whole 4x8x8 slice. The times are simulated.
512 devices in a mesh: dp: 8 (over x, core), vocab: 64 (over y, z).
Axes of the slice: x: 4, y: 8, z: 8, core: 2. Of those that a mesh axis runs over, the one named last changes fastest.
Arguments:
- hidden: bfloat16 [1792, 4608], P('dp'), may hold values from -15 to 15
- out_weight: bfloat16 [4608, 24576], P('dp', 'vocab'), may hold values from -0.09375 to 0.09375
- targets: int32 [1792], P('dp'), may hold values from 0 to 24383
- token_weight: float32 [1792], P('dp'), may hold values from 0.3 to 3
Outputs:
- token_loss: float32 [1792], P('dp')
- hidden_grad: bfloat16 [1792, 4608], P('dp')
- weight_grad: bfloat16 [4608, 24576], P('dp', 'vocab')
All inputs are finite; a program needn't handle non-finite values.
Results may differ from a plain program's by a relative error of at most 0.0085.
Values may be sent and summed in bfloat16 or wider, within the bound.
A program may use at most 64 MiB of HBM per device.

v0:
```python
import jax
import jax.numpy as jnp
from jax import lax
from jax.sharding import Mesh
from jax.sharding import PartitionSpec as P

VOCAB = ("vocab_0", "vocab_1")
softcap = 30.0


def by_axis(array, axes):
    for axis in axes:
        array = lax.psum(array, axis)
    return array


def in_blocks(array, dim, peers):
    before, after = (array.shape[:dim], array.shape[dim + 1 :])
    return jnp.moveaxis(array.reshape(*before, peers, -1, *after), dim, 0)


def sent_and_summed(array, axis, dim):
    blocks = in_blocks(array, dim, lax.axis_size(axis))
    arrived = lax.all_to_all(blocks, axis, split_axis=0, concat_axis=0, tiled=True)
    return arrived.astype(jnp.float32).sum(axis=0)


def from_everyone(array, axis):
    peers = lax.axis_size(axis)
    return lax.all_to_all(
        jnp.broadcast_to(array[None], (peers, *array.shape)), axis, 0, 0, tiled=True
    )


def in_order(blocks, dim):
    blocks = jnp.moveaxis(blocks, 0, dim)
    lengths = blocks.shape
    return blocks.reshape(*lengths[:dim], lengths[dim] * lengths[dim + 1], *lengths[dim + 2 :])


def gather_directly(array, axis, dim):
    blocks = from_everyone(array, axis)
    return in_order(blocks, dim)


def body(hidden, out_weight, targets, token_weight):
    shard_width = out_weight.shape[1]
    row_count = out_weight.shape[0]
    tok_rows = hidden.shape[0]
    vocab_used = shard_width * lax.axis_size(VOCAB) - shard_width // 2
    first_col = lax.axis_index(VOCAB) * shard_width
    col_ids = first_col + jnp.arange(shard_width, dtype=jnp.int32)
    usable = col_ids < vocab_used
    w_full = lax.all_gather(out_weight, "dp", axis=0, tiled=True)
    logits = jnp.dot(hidden, w_full, preferred_element_type=jnp.float32)
    squash = jnp.tanh(logits / softcap)
    capped = softcap * squash
    exp_terms = jnp.where(usable[None, :], jnp.exp(capped), jnp.float32(0.0))
    target_hit = col_ids[None, :] == targets[:, None]
    local_sum = jnp.sum(exp_terms, axis=1)
    local_target = jnp.sum(jnp.where(target_hit, capped, jnp.float32(0.0)), axis=1)
    sums, target_logit = (by_axis(local_sum, VOCAB), by_axis(local_target, VOCAB))
    token_loss = jnp.log(sums) - target_logit
    onehot = jnp.where(target_hit, jnp.float32(1.0), jnp.float32(0.0))
    logit_grad = (
        token_weight[:, None] * (exp_terms / sums[:, None] - onehot) * (1.0 - squash * squash)
    ).astype(jnp.bfloat16)
    contract_cols = (((1,), (1,)), ((), ()))
    partial_grad = lax.dot_general(
        logit_grad, w_full, contract_cols, preferred_element_type=jnp.float32
    )
    share = sent_and_summed(partial_grad.astype(jnp.bfloat16), VOCAB, 1).astype(jnp.bfloat16)
    hidden_grad = lax.all_gather(share, VOCAB, axis=1, tiled=True)
    owned_cols = lax.all_to_all(hidden, "dp", split_axis=1, concat_axis=0, tiled=True)
    every_grad = gather_directly(logit_grad, "dp", 0)
    block_count = owned_cols.shape[0] // tok_rows
    col_blocks = owned_cols.reshape(block_count, tok_rows, row_count)
    grad_blocks = every_grad.reshape(block_count, tok_rows, shard_width)
    block_terms = jnp.einsum(
        "ntr,ntv->nrv", col_blocks, grad_blocks, preferred_element_type=jnp.float32
    ).astype(jnp.bfloat16)
    weight_grad = jnp.sum(block_terms.astype(jnp.float32), axis=0).astype(jnp.bfloat16)
    return (token_loss, hidden_grad, weight_grad)


def solution(mesh):
    torus = Mesh(mesh.devices.reshape(mesh.shape["dp"], 8, 8), ("dp", "vocab_0", "vocab_1"))
    in_specs = (P("dp", None), P("dp", VOCAB), P("dp"), P("dp"))
    out_specs = (P("dp"), P("dp", None), P("dp", VOCAB))
    return jax.shard_map(body, mesh=torus, in_specs=in_specs, out_specs=out_specs, check_vma=False)
```

profile of v0, /device:TPU:4, one launch (start us, length us, event | category | flops | bytes accessed | tf_op | source)
XLA Modules:
  0.0 244.0 jit_solution(11273807396610826851)
XLA Ops:
  7.2 0.0 all-gather.3.cloned.1.call-start
  7.2 0.7 all-gather.3.cloned.1.call-update
  7.9 0.0 all-gather.5.cloned.1.call-start
  8.0 0.0 copy-start
  8.0 0.0 copy-start.1
  8.0 40.0 %all-gather.3.cloned.1.call-done = bf16[4608,384]{1,0:T(8,128)(2,1)} async-done(((bf16[576,384]{1,0:T(8,128)(2,1)}), bf16[4608,384]{1,0:T(8,128)(2,1)}) %all-gather.3.cloned.1.call-update) | async-done | bytes 3538960 | tf_op jit(solution)/shard_map/all_gather | solution.py:54
  48.0 4.1 %fusion.7 = (f32[224]{0:T(256)S(1)}, f32[224]{0:T(256)S(1)}, f32[224,384]{1,0:T(8,128)S(1)}) fusion(pred[384]{0:T(512)(128)(4,1)S(1)} %broadcast_compare_fusion, s32[224]{0:T(256)} %param.6, s32[384]{0:T(512)S(1)} %iota_add_fusion, bf16[224,4608]{1,0:T(8,128)(2,1)} %param.4, bf16[4608,384]{1,0:T(8,128)(2,1)} %all-gather.3.cloned.1.call-done), kind=kOutput, calls=%fused_computation.13 | convolution fusion | flops 793325056 | bytes 5952000 | tf_op jit(solution)/shard_map/dot_general | solution.py:55
  52.1 17.0 %all-reduce.1 = (f32[224]{0:T(256)S(1)}, f32[224]{0:T(256)S(1)}) all-reduce(f32[224]{0:T(256)S(1)} %get-tuple-element.7, f32[224]{0:T(256)S(1)} %get-tuple-element.6), channel_id=1, replica_groups=mesh['dp'=8,'vocab_0'=8,'vocab_1'=8] {'vocab_0'}, use_global_device_ids=true, to_apply=%region_4.5 | all-reduce | flops 448 | bytes 3584 | tf_op jit(solution)/shard_map/psum | solution.py:13
  69.1 18.1 %all-reduce = (f32[224]{0:T(256)S(1)}, f32[224]{0:T(256)S(1)}) all-reduce(f32[224]{0:T(256)S(1)} %get-tuple-element.10, f32[224]{0:T(256)S(1)} %get-tuple-element.11), channel_id=1, replica_groups=mesh['dp'=8,'vocab_0'=8,'vocab_1'=8] {'vocab_1'}, use_global_device_ids=true, to_apply=%region_5.6 | all-reduce | flops 448 | bytes 3584 | tf_op jit(solution)/shard_map/psum | solution.py:13
  87.2 0.0 copy-done
  87.2 0.0 copy-done.1
  87.2 0.2 fusion.6
  87.4 3.4 %convolution_convert_fusion = bf16[224,4608]{1,0:T(8,128)(2,1)S(1)} fusion(bf16[224,384]{1,0:T(8,128)(2,1)S(1)} %fusion.6, bf16[4608,384]{1,0:T(8,128)(2,1)} %all-gather.3.cloned.1.call-done), kind=kOutput, calls=%fused_computation | convolution fusion | flops 793755648 | bytes 5775360 | tf_op jit(solution)/shard_map/dot_general | solution.py:69
  90.8 2.4 copy.9
  93.2 60.9 %all_to_all.26 = bf16[64,224,72]{1,2,0:T(8,128)(2,1)S(1)} all-to-all(bf16[64,224,72]{1,2,0:T(8,128)(2,1)} %bitcast.12), channel_id=1, replica_groups=mesh['dp'=8,'vocab_0'=8,'vocab_1'=8] {'vocab_0','vocab_1'}, dimensions={0} | all-to-all | bytes 4128768 | tf_op jit(solution)/shard_map/all_to_all | solution.py:24
  154.1 1.0 reduce_sum.46
  155.1 0.0 all-gather.5.cloned.1.call-update
  155.1 3.6 %all_to_all.20 = bf16[224,8,576]{2,1,0:T(8,128)(2,1)S(1)} reshape(bf16[224,4608]{1,0:T(8,128)(2,1)} %param.4) | data formatting | bytes 4128768 | tf_op jit(solution)/shard_map/all_to_all | solution.py:74
  158.7 0.3 copy.10
  159.0 31.3 %all_to_all.27 = bf16[224,8,576]{2,0,1:T(8,128)(2,1)S(1)} all-to-all(bf16[224,8,576]{2,0,1:T(8,128)(2,1)S(1)} %copy.10), channel_id=1, replica_groups=mesh['dp'=8,'vocab_0'=8,'vocab_1'=8] {'dp'}, dimensions={1} | all-to-all | bytes 4128768 | tf_op jit(solution)/shard_map/all_to_all | solution.py:74
  190.2 1.2 broadcast_in_dim.34
  191.4 6.8 %all-to-all-start.1 = ((bf16[8,224,384]{2,1,0:T(8,128)(2,1)}), bf16[8,224,384]{2,1,0:T(8,128)(2,1)}, u32[]{:S(2)}, u32[]{:S(2)}) async-start(bf16[8,224,384]{2,1,0:T(8,128)(2,1)} %broadcast_in_dim.34), calls=%async_computation.1 | async-start | bytes 2752512 | tf_op jit(solution)/shard_map/all_to_all | solution.py:30
  198.3 0.6 log_subtract_fusion
  198.8 15.8 %all-to-all-done.1 = bf16[8,224,384]{2,1,0:T(8,128)(2,1)} async-done(((bf16[8,224,384]{2,1,0:T(8,128)(2,1)}), bf16[8,224,384]{2,1,0:T(8,128)(2,1)}, u32[]{:S(2)}, u32[]{:S(2)}) %all-to-all-start.1) | async-done | bytes 1376288 | tf_op jit(solution)/shard_map/all_to_all | solution.py:30
  214.7 3.6 %convert_reduce_fusion = bf16[384,576]{0,1:T(8,128)(2,1)} fusion(bf16[8,224,384]{2,1,0:T(8,128)(2,1)} %all-to-all-done.1, bf16[224,8,576]{2,0,1:T(8,128)(2,1)S(1)} %all_to_all.27), kind=kOutput, calls=%fused_computation.1 | convolution fusion | flops 796041216 | bytes 3883008 | tf_op jit(solution)/shard_map/ntr,ntv->nrv/dot_general | solution.py:79
  218.3 14.7 %all-gather.5.cloned.1.call-done = bf16[224,4608]{0,1:T(8,128)(2,1)} async-done(((bf16[224,72]{0,1:T(8,128)(2,1)}), bf16[224,4608]{0,1:T(8,128)(2,1)}) %all-gather.5.cloned.1.call-update) | async-done | bytes 2064400 | tf_op jit(solution)/shard_map/all_gather | solution.py:73
  233.0 4.1 %copy.11 = bf16[224,4608]{1,0:T(8,128)(2,1)} copy(bf16[224,4608]{0,1:T(8,128)(2,1)} %all-gather.5.cloned.1.call-done) | data formatting | bytes 4128768
  (2 shorter events, 0.0 us)
Async XLA Ops:
  7.2 40.9 %all-gather.3.cloned.1.call-start = ((), (), s32[]{:S(2)}) async-start(), calls=%async_computation.3 | async-start | bytes 3981312 | tf_op jit(solution)/shard_map/all_gather | solution.py:54
  7.9 225.1 %all-gather.5.cloned.1.call-start = ((), (), s32[]{:S(2)}) async-start(), calls=%async_computation.4 | async-start | bytes 2396160 | tf_op jit(solution)/shard_map/all_gather | solution.py:73
  8.0 79.2 %copy-start = (s32[224]{0:T(256)S(1)}, s32[224]{0:T(256)}, u32[]{:S(2)}) copy-start(s32[224]{0:T(256)} %param.6) | copy-start | bytes 2692
  8.0 79.2 %copy-start.1 = (f32[224]{0:T(256)S(1)}, f32[224]{0:T(256)}, u32[]{:S(2)}) copy-start(f32[224]{0:T(256)} %param.7) | copy-start | bytes 2692
  191.4 23.2 %all-to-all-start.1 = ((bf16[8,224,384]{2,1,0:T(8,128)(2,1)}), bf16[8,224,384]{2,1,0:T(8,128)(2,1)}, u32[]{:S(2)}, u32[]{:S(2)}) async-start(bf16[8,224,384]{2,1,0:T(8,128)(2,1)} %broadcast_in_dim.34), calls=%async_computation.1 | async-start | bytes 2752512 | tf_op jit(solution)/shard_map/all_to_all | solution.py:30
Sparse Core Ops, SparseCore 0:
  10.1 37.8 all-gather.2
  155.2 77.6 all-gather.4
where the time goes:
time: 244 us
  blocking collectives  127 us (52%)
  waiting for transfers between devices  71.2 us (29%)
  between operations  14.1 us (6%)
  local copies, waits for them, and re-layouts  11.6 us (5%)
  matrix products  11.1 us (5%)
  starting transfers between devices  6.9 us (3%)
    all_to_all x1, blocking collectives, sent_and_summed(): lax.all_to_all(blocks, axis, split_axis=0, concat_axis=0, tiled=True)  60.9 us
    all_gather x1, waiting for transfers between devices, body(): w_full = lax.all_gather(out_weight, 'dp', axis=0, tiled=True)  40 us
    psum x2, blocking collectives, by_axis(): array = lax.psum(array, axis)  35.1 us
    all_to_all x1, blocking collectives, body(): lax.all_to_all(hidden, 'dp', split_axis=1, concat_axis=0, tiled=True)  31.3 us
    all_to_all x1, waiting for transfers between devices, from_everyone(): lax.all_to_all(jnp.broadcast_to(array[None], (peers, *array.shape)), axis...  15.8 us
    all_gather x1, waiting for transfers between devices, body(): hidden_grad = lax.all_gather(share, VOCAB, axis=1, tiled=True)  14.7 us
    all_to_all x1, starting transfers between devices, from_everyone(): lax.all_to_all(jnp.broadcast_to(array[None], (peers, *array.shape)), axis...  6.83 us
  transfers between devices with their start and end apart: 3, of which 3 were waited for; matrix products, arithmetic and copies ran while one was open for 2% of the time, Pallas kernels for 0%

commit v1 on v0

--- a/solution.py
+++ b/solution.py
@@ -10,7 +10,7 @@
 
 def by_axis(array, axes):
     for axis in axes:
-        array = lax.psum(array, axis)
+        array = jnp.sum(lax.all_gather(array, axis), axis=0)
     return array
 
 

time: 244 us -> 270 us (1.11)
  blocking collectives: 127 us -> 146 us
  local copies, waits for them, and re-layouts: 11.6 us -> 15.5 us
    unnamed x0 -> x2, blocking collectives: none -> 60.4 us
    psum x2 -> x0, blocking collectives: 35.1 us -> none  [by_axis(): array = lax.psum(array, axis)]
    all_to_all x1, blocking collectives: 60.9 us -> 53.9 us  [sent_and_summed(): lax.all_to_all(blocks, axis, split_axis=0, concat_axis=0, tiled=True)]
    all_gather x1, waiting for transfers between devices: 14.7 us -> 20.4 us  [body(): hidden_grad = lax.all_gather(share, VOCAB, axis=1, tiled=True)]
    all_gather x1, waiting for transfers between devices: 40 us -> 36.2 us  [body(): w_full = lax.all_gather(out_weight, 'dp', axis=0, tiled=True)]
    unnamed x5 -> x15, local copies, waits for them, and re-layouts: 4.16 us -> 7.78 us
  transfers between devices with their start and end apart: 3 -> 3, of which waited for: 3 -> 3; matrix products, arithmetic and copies ran while one was open for 2% -> 3% of each run, Pallas kernels for 0% -> 0%
where the time goes in v1:
time: 270 us; the launch traced here: 269 us
  blocking collectives  146 us (54%)
  waiting for transfers between devices  73 us (27%)
  local copies, waits for them, and re-layouts  15.5 us (6%)
  between operations  15.4 us (6%)
  matrix products  11.2 us (4%)
  starting transfers between devices  6.9 us (3%)
    unnamed x2, blocking collectives  60.4 us
    all_to_all x1, blocking collectives, sent_and_summed(): lax.all_to_all(blocks, axis, split_axis=0, concat_axis=0, tiled=True)  53.9 us
    all_gather x1, waiting for transfers between devices, body(): w_full = lax.all_gather(out_weight, 'dp', axis=0, tiled=True)  36.2 us
    all_to_all x1, blocking collectives, body(): lax.all_to_all(hidden, 'dp', split_axis=1, concat_axis=0, tiled=True)  31.3 us
    all_gather x1, waiting for transfers between devices, body(): hidden_grad = lax.all_gather(share, VOCAB, axis=1, tiled=True)  20.4 us
    all_to_all x1, waiting for transfers between devices, from_everyone(): lax.all_to_all(jnp.broadcast_to(array[None], (peers, *array.shape)), axis...  15.7 us
    unnamed x15, local copies, waits for them, and re-layouts  7.78 us
    all_to_all x1, starting transfers between devices, from_everyone(): lax.all_to_all(jnp.broadcast_to(array[None], (peers, *array.shape)), axis...  6.83 us
  transfers between devices with their start and end apart: 3, of which 3 were waited for; matrix products, arithmetic and copies ran while one was open for 3% of the time, Pallas kernels for 0%

profile of v1, /device:TPU:4, one launch (start us, length us, event | category | flops | bytes accessed | tf_op | source)
XLA Modules:
  0.0 269.4 jit_solution(11211514790460075732)
XLA Ops:
  7.2 0.0 all-gather.7.cloned.1.call-start
  7.2 0.7 all-gather.7.cloned.1.call-update
  7.9 0.0 all-gather.9.cloned.1.call-start
  8.0 1.3 dynamic-slice.1
  9.2 1.3 dynamic-slice
  11.8 0.0 copy-start
  11.8 0.0 copy-start.1
  11.8 36.2 %all-gather.7.cloned.1.call-done = bf16[4608,384]{1,0:T(8,128)(2,1)} async-done(((bf16[576,384]{1,0:T(8,128)(2,1)}), bf16[4608,384]{1,0:T(8,128)(2,1)}) %all-gather.7.cloned.1.call-update) | async-done | bytes 3538960 | tf_op jit(solution)/shard_map/all_gather | solution.py:54
  48.0 4.1 %fusion.7 = (f32[224]{0:T(256)S(1)}, f32[224]{0:T(256)S(1)}, f32[224,384]{1,0:T(8,128)S(1)}) fusion(pred[384]{0:T(512)(128)(4,1)S(1)} %broadcast_compare_fusion, s32[224]{0:T(256)} %param.6, s32[384]{0:T(512)S(1)} %iota_add_fusion, bf16[224,4608]{1,0:T(8,128)(2,1)} %param.4, bf16[4608,384]{1,0:T(8,128)(2,1)} %all-gather.7.cloned.1.call-done), kind=kOutput, calls=%fused_computation.13 | convolution fusion | flops 793325056 | bytes 5952000 | tf_op jit(solution)/shard_map/dot_general | solution.py:55
  52.1 0.3 dynamic-update-slice
  52.4 0.3 dynamic-update-slice.2
  52.7 29.6 %all-reduce.5 = (f32[1792]{0:T(1024)S(1)}, f32[1792]{0:T(1024)S(1)}) all-reduce(f32[1792]{0:T(1024)S(1)} %dynamic-update-slice.2, f32[1792]{0:T(1024)S(1)} %dynamic-update-slice), channel_id=4, replica_groups=mesh['dp'=8,'vocab_0'=8,'vocab_1'=8] {'vocab_0'}, use_global_device_ids=true, to_apply=%add.2 | all-reduce | flops 3584 | bytes 28672
  82.3 0.1 reshape.28
  82.4 0.1 reshape.26
  82.5 0.3 dynamic-update-slice.3
  82.8 0.3 dynamic-update-slice.1
  83.0 30.8 %all-reduce.4 = (f32[1792]{0:T(1024)S(1)}, f32[1792]{0:T(1024)S(1)}) all-reduce(f32[1792]{0:T(1024)S(1)} %dynamic-update-slice.3, f32[1792]{0:T(1024)S(1)} %dynamic-update-slice.1), channel_id=5, replica_groups=mesh['dp'=8,'vocab_0'=8,'vocab_1'=8] {'vocab_1'}, use_global_device_ids=true, to_apply=%add.3 | all-reduce | flops 3584 | bytes 28672
  113.8 0.1 reshape.27
  113.9 0.0 copy-done
  113.9 0.0 copy-done.1
  113.9 0.2 fusion.6
  114.1 3.4 %convolution_convert_fusion = bf16[224,4608]{1,0:T(8,128)(2,1)S(1)} fusion(bf16[224,384]{1,0:T(8,128)(2,1)S(1)} %fusion.6, bf16[4608,384]{1,0:T(8,128)(2,1)} %all-gather.7.cloned.1.call-done), kind=kOutput, calls=%fused_computation | convolution fusion | flops 793755648 | bytes 5775360 | tf_op jit(solution)/shard_map/dot_general | solution.py:69
  117.5 2.4 copy.12
  119.9 53.9 %all_to_all.26 = bf16[64,224,72]{1,2,0:T(8,128)(2,1)S(1)} all-to-all(bf16[64,224,72]{1,2,0:T(8,128)(2,1)} %bitcast.14), channel_id=1, replica_groups=mesh['dp'=8,'vocab_0'=8,'vocab_1'=8] {'vocab_0','vocab_1'}, dimensions={0} | all-to-all | bytes 4128768 | tf_op jit(solution)/shard_map/all_to_all | solution.py:24
  173.8 1.0 reduce_sum.86
  174.8 0.0 all-gather.9.cloned.1.call-update
  174.8 3.6 %all_to_all.20 = bf16[224,8,576]{2,1,0:T(8,128)(2,1)S(1)} reshape(bf16[224,4608]{1,0:T(8,128)(2,1)} %param.4) | data formatting | bytes 4128768 | tf_op jit(solution)/shard_map/all_to_all | solution.py:74
  178.4 0.3 copy.13
  178.7 31.3 %all_to_all.27 = bf16[224,8,576]{2,0,1:T(8,128)(2,1)S(1)} all-to-all(bf16[224,8,576]{2,0,1:T(8,128)(2,1)S(1)} %copy.13), channel_id=1, replica_groups=mesh['dp'=8,'vocab_0'=8,'vocab_1'=8] {'dp'}, dimensions={1} | all-to-all | bytes 4128768 | tf_op jit(solution)/shard_map/all_to_all | solution.py:74
  210.0 1.2 broadcast_in_dim.34
  211.2 6.8 %all-to-all-start.1 = ((bf16[8,224,384]{2,1,0:T(8,128)(2,1)}), bf16[8,224,384]{2,1,0:T(8,128)(2,1)}, u32[]{:S(2)}, u32[]{:S(2)}) async-start(bf16[8,224,384]{2,1,0:T(8,128)(2,1)} %broadcast_in_dim.34), calls=%async_computation.1 | async-start | bytes 2752512 | tf_op jit(solution)/shard_map/all_to_all | solution.py:30
  218.0 0.1 reshape.29
  218.1 0.6 log_subtract_fusion
  218.7 15.7 %all-to-all-done.1 = bf16[8,224,384]{2,1,0:T(8,128)(2,1)} async-done(((bf16[8,224,384]{2,1,0:T(8,128)(2,1)}), bf16[8,224,384]{2,1,0:T(8,128)(2,1)}, u32[]{:S(2)}, u32[]{:S(2)}) %all-to-all-start.1) | async-done | bytes 1376288 | tf_op jit(solution)/shard_map/all_to_all | solution.py:30
  234.4 3.7 %convert_reduce_fusion = bf16[384,576]{0,1:T(8,128)(2,1)} fusion(bf16[8,224,384]{2,1,0:T(8,128)(2,1)} %all-to-all-done.1, bf16[224,8,576]{2,0,1:T(8,128)(2,1)S(1)} %all_to_all.27), kind=kOutput, calls=%fused_computation.1 | convolution fusion | flops 796041216 | bytes 3883008 | tf_op jit(solution)/shard_map/ntr,ntv->nrv/dot_general | solution.py:79
  238.1 20.4 %all-gather.9.cloned.1.call-done = bf16[224,4608]{0,1:T(8,128)(2,1)} async-done(((bf16[224,72]{0,1:T(8,128)(2,1)}), bf16[224,4608]{0,1:T(8,128)(2,1)}) %all-gather.9.cloned.1.call-update) | async-done | bytes 2064400 | tf_op jit(solution)/shard_map/all_gather | solution.py:73
  258.4 4.1 %copy.14 = bf16[224,4608]{1,0:T(8,128)(2,1)} copy(bf16[224,4608]{0,1:T(8,128)(2,1)} %all-gather.9.cloned.1.call-done) | data formatting | bytes 4128768
  (10 shorter events, 0.1 us)
Async XLA Ops:
  7.2 40.9 %all-gather.7.cloned.1.call-start = ((), (), s32[]{:S(2)}) async-start(), calls=%async_computation.3 | async-start | bytes 3981312 | tf_op jit(solution)/shard_map/all_gather | solution.py:54
  7.9 250.6 %all-gather.9.cloned.1.call-start = ((), (), s32[]{:S(2)}) async-start(), calls=%async_computation.4 | async-start | bytes 2396160 | tf_op jit(solution)/shard_map/all_gather | solution.py:73
  11.8 102.1 %copy-start = (s32[224]{0:T(256)S(1)}, s32[224]{0:T(256)}, u32[]{:S(2)}) copy-start(s32[224]{0:T(256)} %param.6) | copy-start | bytes 2692
  11.8 102.1 %copy-start.1 = (f32[224]{0:T(256)S(1)}, f32[224]{0:T(256)}, u32[]{:S(2)}) copy-start(f32[224]{0:T(256)} %param.7) | copy-start | bytes 2692
  211.2 23.2 %all-to-all-start.1 = ((bf16[8,224,384]{2,1,0:T(8,128)(2,1)}), bf16[8,224,384]{2,1,0:T(8,128)(2,1)}, u32[]{:S(2)}, u32[]{:S(2)}) async-start(bf16[8,224,384]{2,1,0:T(8,128)(2,1)} %broadcast_in_dim.34), calls=%async_computation.1 | async-start | bytes 2752512 | tf_op jit(solution)/shard_map/all_to_all | solution.py:30
Sparse Core Ops, SparseCore 0:
  10.1 37.8 all-gather.6
  175.0 83.4 all-gather.8
